TPU v7x, 32 devices: a whole 2x2x4 slice. The times are simulated.
32 devices in a mesh: gx: 2 (over x), gy: 4 (over y, core), gz: 4 (over z).
Axes of the slice: x: 2, y: 2, z: 4, core: 2. Of those that a mesh axis runs over, the one named last changes fastest.
Arguments:
- rhs: float32 [8, 8, 2, 16, 512], P(None, None, 'gx', 'gy', 'gz'), as said below
- blocks: bfloat16 [7, 8, 8, 2, 16, 512], P(None, None, None, 'gx', 'gy', 'gz'), as said below
Outputs:
- basis: float32 [4, 8, 8, 2, 16, 512], P(None, None, None, 'gx', 'gy', 'gz')
- hess: float32 [4, 8, 3, 8], replicated
Inputs may be any that keep to these rules, and one draw needn't show every extreme that they name: `rhs`: each cell's value is a random draw times a positive scale that varies smoothly over the grid. The operator couples each cell only to itself and its six face neighbours; its blocks are full and the block Krylov spaces keep full rank.
All inputs are finite; a program needn't handle non-finite values.
Results may differ from a plain program's by a relative error of at most 0.001.
Values sent between devices are 32-bit elements; how exact they have to be, the bound alone decides.
A program may use at most 64 MiB of HBM per device.

v0:
```python
import jax
import jax.numpy as jnp
from jax import lax
from jax.sharding import PartitionSpec as P

RHS = 8
ITERS = 3
HIGH = lax.Precision.HIGHEST


def with_halo(block, sides, width):
    for axis, dim in sides:
        count = lax.axis_size(axis)
        forward = [(i, i + 1) for i in range(count - 1)]
        backward = [(target, source) for source, target in forward]
        low = lax.ppermute(
            lax.slice_in_dim(block, block.shape[dim] - width, None, axis=dim), axis, forward
        )
        high = lax.ppermute(lax.slice_in_dim(block, 0, width, axis=dim), axis, backward)
        block = jnp.concatenate([low, block, high], axis=dim)
    return block


def couple(padded, blocks):
    views = [
        padded[:, :, 1:-1, 1:-1, 1:-1],
        padded[:, :, 2:, 1:-1, 1:-1],
        padded[:, :, :-2, 1:-1, 1:-1],
        padded[:, :, 1:-1, 2:, 1:-1],
        padded[:, :, 1:-1, :-2, 1:-1],
        padded[:, :, 1:-1, 1:-1, 2:],
        padded[:, :, 1:-1, 1:-1, :-2],
    ]
    total = jnp.zeros(views[0].shape, jnp.float32)
    for k in range(7):
        for j in range(views[0].shape[0]):
            column = blocks[k, :, j].astype(jnp.float32)
            total = total + column[:, None] * views[k][j][None]
    return total


def stencil(field, blocks):
    padded = with_halo(field, (("gx", 2), ("gy", 3), ("gz", 4)), 1)
    return couple(padded, blocks)


def pair(first, second):
    return jnp.einsum("arxyz,asxyz->rs", first, second, precision=HIGH)


def mix(field, matrix):
    return jnp.einsum("asxyz,sr->arxyz", field, matrix, precision=HIGH)


def normalizer(gram, eye):
    lower = jnp.linalg.cholesky(gram)
    inverse = lax.linalg.triangular_solve(lower, eye, left_side=True, lower=True)
    return (inverse.T, lower.T)


def shards(rhs, blocks):
    eye = jnp.eye(RHS, dtype=jnp.float32)
    hess = jnp.zeros((ITERS + 1, RHS, ITERS, RHS), jnp.float32)
    first_pair = None
    raw_image = stencil(rhs, blocks)
    gram_start, cross, square = lax.psum(
        (pair(rhs, rhs), pair(rhs, raw_image), pair(raw_image, raw_image)), ("gx", "gy", "gz")
    )
    scale, upper = normalizer(gram_start, eye)
    basis = [mix(rhs, scale)]
    images = [mix(raw_image, scale)]
    first_coeff = jnp.dot(jnp.dot(scale.T, cross, precision=HIGH), scale, precision=HIGH)
    first_gram = jnp.dot(jnp.dot(scale.T, square, precision=HIGH), scale, precision=HIGH)
    first_pair = (first_coeff, first_gram)
    for step in range(ITERS):
        image = images[step]
        if step == 0 and first_pair is not None:
            coeffs = [first_pair[0]]
            gram = first_pair[1]
        else:
            stacked = jnp.stack(basis + [image])
            partial_sums = jnp.einsum("karxyz,asxyz->krs", stacked, image, precision=HIGH)
            summed = lax.psum(partial_sums, ("gx", "gy", "gz"))
            coeffs = [summed[index] for index in range(len(basis))]
            gram = summed[len(basis)]
        rest = image
        for vector, coeff in zip(basis, coeffs):
            gram = gram - jnp.dot(coeff.T, coeff, precision=HIGH)
            rest = rest - mix(vector, coeff)
        scale, upper = normalizer(gram, eye)
        fresh = mix(rest, scale)
        basis.append(fresh)
        for index, coeff in enumerate(coeffs):
            hess = hess.at[index, :, step, :].set(coeff)
        hess = hess.at[step + 1, :, step, :].set(upper)
        if step + 1 < ITERS:
            images.append(stencil(fresh, blocks))
    return (jnp.stack(basis), hess)


def solution(mesh):
    placed = (P(None, None, "gx", "gy", "gz"), P(None, None, None, "gx", "gy", "gz"))
    return jax.shard_map(
        shards,
        mesh=mesh,
        in_specs=placed,
        out_specs=(P(None, None, None, "gx", "gy", "gz"), P()),
        check_vma=False,
    )
```

profile of v0, /device:TPU:0, one launch (start us, length us, event | category | flops | bytes accessed | tf_op | source)
XLA Modules:
  0.0 246.0 jit_solution(17078392354189909345)
XLA Ops:
  0.6 1.0 copy.203
  1.6 4.9 %collective-permute-start.1 = (f32[8,8,1,4,128]{4,1,3,2,0:T(8,128)S(1)}, f32[8,8,1,4,128]{4,1,3,2,0:T(8,128)S(1)}, u32[]{:S(2)}, u32[]{:S(2)}) collective-permute-start(f32[8,8,1,4,128]{4,1,3,2,0:T(8,128)S(1)} %copy.203), channel_id=1, source_target_pairs={{0,16},{1,17},{2,18},{3,19},{4,20},{5,21},{6,22},{7,23},{8,24},{9,... | collective-permute-start | bytes 393224 | tf_op jit(solution)/shard_map/ppermute | solution.py:16
  6.5 1.3 collective-permute-start
  7.8 0.9 bitcast_convert_fusion.53
  10.2 3.1 %collective-permute-done = f32[8,8,1,4,128]{4,1,3,2,0:T(8,128)S(1)} collective-permute-done((f32[8,8,1,4,128]{4,1,3,2,0:T(8,128)S(1)}, f32[8,8,1,4,128]{4,1,3,2,0:T(8,128)S(1)}, u32[]{:S(2)}, u32[]{:S(2)}) %collective-permute-start) | collective-permute-done | bytes 131104 | tf_op jit(solution)/shard_map/ppermute | solution.py:19
  13.4 1.3 collective-permute-start.2
  14.7 3.0 %collective-permute-start.3 = (f32[8,8,3,1,128]{4,1,3,2,0:T(8,128)S(1)}, f32[8,8,3,1,128]{4,1,3,2,0:T(8,128)S(1)}, u32[]{:S(2)}, u32[]{:S(2)}) collective-permute-start(f32[8,8,3,1,128]{4,1,3,2,0:T(8,128)S(1)} %get-tuple-element.285), channel_id=1, source_target_pairs={{0,4},{4,8},{8,12},{1,5},{5,9},{9,13},{2,6},{6,10},{10,14},{3,7},{... | collective-permute-start | bytes 294920 | tf_op jit(solution)/shard_map/ppermute | solution.py:16
  18.9 0.9 copy.278
  19.8 3.5 %collective-permute-start.5 = (f32[8,8,3,6,1]{1,0,4,3,2:T(8,128)S(1)}, f32[8,8,3,6,1]{1,0,4,3,2:T(8,128)S(1)}, u32[]{:S(2)}, u32[]{:S(2)}) collective-permute-start(f32[8,8,3,6,1]{1,0,4,3,2:T(8,128)S(1)} %copy.278), channel_id=1, source_target_pairs={{0,1},{1,2},{2,3},{4,5},{5,6},{6,7},{8,9},{9,10},{10,11},{12,13},{... | collective-permute-start | bytes 13832 | tf_op jit(solution)/shard_map/ppermute | solution.py:16
  24.2 1.3 collective-permute-start.4
  25.6 0.9 copy.209
  26.7 4.0 %collective-permute-done.4 = f32[8,8,3,6,1]{1,0,4,3,2:T(8,128)S(1)} collective-permute-done((f32[8,8,3,6,1]{1,0,4,3,2:T(8,128)S(1)}, f32[8,8,3,6,1]{1,0,4,3,2:T(8,128)S(1)}, u32[]{:S(2)}, u32[]{:S(2)}) %collective-permute-start.4) | collective-permute-done | bytes 4640 | tf_op jit(solution)/shard_map/ppermute | solution.py:19
  30.7 0.9 copy.207
  31.8 1.0 multiply_add_fusion.2
  33.6 41.6 %all-reduce.1 = (f32[8,8]{0,1:T(8,128)S(1)}, f32[8,8]{1,0:T(8,128)S(1)}, f32[8,8]{0,1:T(8,128)S(1)}) all-reduce(f32[8,8]{0,1:T(8,128)S(1)} %convolution_bitcast_fusion.13, f32[8,8]{1,0:T(8,128)S(1)} %convolution_bitcast_fusion.12, f32[8,8]{0,1:T(8,128)S(1)} %convolution_bitcast_fusion.11), channel_id=1, replica_groups=mesh['gx'=2,'gy'=4,'gz'=4] {'gx','gy','gz'}, use_global_device_ids=true, to_apply=%region_0.0 | all-reduce | flops 192 | bytes 1536 | tf_op jit(solution)/shard_map/psum | solution.py:66
  83.0 1.3 collective-permute-start.6
  84.3 4.6 %collective-permute-start.7 = (f32[8,8,1,4,128]{4,1,3,0,2:T(8,128)S(1)}, f32[8,8,1,4,128]{4,1,3,0,2:T(8,128)S(1)}, u32[]{:S(2)}, u32[]{:S(2)}) collective-permute-start(f32[8,8,1,4,128]{4,1,3,0,2:T(8,128)S(1)} %bitcast.786), channel_id=1, source_target_pairs={{0,16},{1,17},{2,18},{3,19},{4,20},{5,21},{6,22},{7,23},{8,24},{9,... | collective-permute-start | bytes 393224 | tf_op jit(solution)/shard_map/ppermute | solution.py:16
  90.8 2.8 %and_reduce_fusion = (pred[]{:T(512)}, pred[]{:T(512)}) fusion(s32[4]{0:T(128)S(1)} %copy-done.3, s32[1]{0:T(128)} %constant.288.clone.1, s32[1]{0:T(128)} %get-tuple-element.366, s32[1]{0:T(128)} %get-tuple-element.365, s32[1]{0:T(128)} %slice.1472, s32[1]{0:T(128)S(1)} %bitcast.825), kind=kLoop, calls=%fused_computation.849 | loop fusion | flops 54 | bytes 38 | tf_op jit(solution)/shard_map/reduce.18
  93.7 1.3 collective-permute-start.8
  95.0 3.0 %collective-permute-start.9 = (f32[8,8,3,1,128]{4,1,3,0,2:T(8,128)S(1)}, f32[8,8,3,1,128]{4,1,3,0,2:T(8,128)S(1)}, u32[]{:S(2)}, u32[]{:S(2)}) collective-permute-start(f32[8,8,3,1,128]{4,1,3,0,2:T(8,128)S(1)} %get-tuple-element.283), channel_id=1, source_target_pairs={{0,4},{4,8},{8,12},{1,5},{5,9},{9,13},{2,6},{6,10},{10,14},{3,7},{... | collective-permute-start | bytes 294920 | tf_op jit(solution)/shard_map/ppermute | solution.py:16
  99.2 0.9 copy.218
  100.1 2.2 collective-permute-start.11
  103.2 1.3 collective-permute-start.10
  104.6 0.9 copy.219
  105.7 3.7 %collective-permute-done.10 = f32[8,8,3,6,1]{1,0,4,3,2:T(8,128)S(1)} collective-permute-done((f32[8,8,3,6,1]{1,0,4,3,2:T(8,128)S(1)}, f32[8,8,3,6,1]{1,0,4,3,2:T(8,128)S(1)}, u32[]{:S(2)}, u32[]{:S(2)}) %collective-permute-start.10) | collective-permute-done | bytes 4640 | tf_op jit(solution)/shard_map/ppermute | solution.py:19
  109.4 0.9 copy.217
  110.6 1.1 multiply_add_fusion.1
  111.7 1.6 convolution_bitcast_fusion.7
  113.3 42.8 %psum.38 = f32[3,8,8]{2,1,0:T(8,128)S(1)} all-reduce(f32[3,8,8]{2,1,0:T(8,128)S(1)} %convolution_bitcast_fusion.7), channel_id=1, replica_groups=mesh['gx'=2,'gy'=4,'gz'=4] {'gx','gy','gz'}, use_global_device_ids=true, to_apply=%region_5.8 | all-reduce | flops 192 | bytes 1536 | tf_op jit(solution)/shard_map/psum | solution.py:83
  159.8 1.3 fusion.3
  161.4 1.3 collective-permute-start.12
  162.7 4.6 %collective-permute-start.13 = (f32[8,8,1,4,128]{4,1,3,0,2:T(8,128)S(1)}, f32[8,8,1,4,128]{4,1,3,0,2:T(8,128)S(1)}, u32[]{:S(2)}, u32[]{:S(2)}) collective-permute-start(f32[8,8,1,4,128]{4,1,3,0,2:T(8,128)S(1)} %bitcast.803), channel_id=1, source_target_pairs={{0,16},{1,17},{2,18},{3,19},{4,20},{5,21},{6,22},{7,23},{8,24},{9,... | collective-permute-start | bytes 393224 | tf_op jit(solution)/shard_map/ppermute | solution.py:16
  167.3 1.3 fusion.499
  168.7 1.1 collective-permute-done.13
  169.8 1.3 collective-permute-start.14
  171.1 3.0 %collective-permute-start.15 = (f32[8,8,3,1,128]{4,1,3,0,2:T(8,128)S(1)}, f32[8,8,3,1,128]{4,1,3,0,2:T(8,128)S(1)}, u32[]{:S(2)}, u32[]{:S(2)}) collective-permute-start(f32[8,8,3,1,128]{4,1,3,0,2:T(8,128)S(1)} %get-tuple-element.281), channel_id=1, source_target_pairs={{0,4},{4,8},{8,12},{1,5},{5,9},{9,13},{2,6},{6,10},{10,14},{3,7},{... | collective-permute-start | bytes 294920 | tf_op jit(solution)/shard_map/ppermute | solution.py:16
  175.3 0.9 copy.230
  176.2 2.2 collective-permute-start.17
  179.3 1.3 collective-permute-start.16
  180.7 0.9 copy.231
  181.8 3.7 %collective-permute-done.16 = f32[8,8,3,6,1]{1,0,4,3,2:T(8,128)S(1)} collective-permute-done((f32[8,8,3,6,1]{1,0,4,3,2:T(8,128)S(1)}, f32[8,8,3,6,1]{1,0,4,3,2:T(8,128)S(1)}, u32[]{:S(2)}, u32[]{:S(2)}) %collective-permute-start.16) | collective-permute-done | bytes 4640 | tf_op jit(solution)/shard_map/ppermute | solution.py:19
  185.5 0.9 copy.229
  186.7 1.0 multiply_add_fusion
  187.8 1.6 convolution_bitcast_fusion.6
  189.4 44.9 %psum.39 = f32[4,8,8]{2,1,0:T(8,128)S(1)} all-reduce(f32[4,8,8]{2,1,0:T(8,128)S(1)} %convolution_bitcast_fusion.6), channel_id=1, replica_groups=mesh['gx'=2,'gy'=4,'gz'=4] {'gx','gy','gz'}, use_global_device_ids=true, to_apply=%region_6.9 | all-reduce | flops 256 | bytes 2048 | tf_op jit(solution)/shard_map/psum | solution.py:83
  238.6 1.1 fusion.7
  240.0 0.9 copy.245
  240.9 3.3 %fusion.498 = f32[4,8,3,8]{3,1,2,0:T(8,128)} fusion(f32[4,8,3,8]{3,1,2,0:T(8,128)} %copy-done.2, s32[]{:T(128)} %bitcast.379, s32[]{:T(128)} %bitcast.380, f32[4,8,8]{2,1,0:T(8,128)S(1)} %psum.39, pred[]{:T(512)} %get-tuple-element.118), kind=kLoop, calls=%fused_computation.797 | loop fusion | flops 64 | bytes 9984 | tf_op jit(solution)/shard_map/scatter | solution.py:94
  (149 shorter events, 30.1 us)
Async XLA Ops:
  0.6 8.1 %copy-start.1 = (bf16[7,8,8,1,4,128]{5,4,3,2,1,0:T(4,128)(2,1)S(1)}, bf16[7,8,8,1,4,128]{5,4,3,2,1,0:T(4,128)(2,1)}, u32[]{:S(2)}) copy-start(bf16[7,8,8,1,4,128]{5,4,3,2,1,0:T(4,128)(2,1)} %param.24) | copy-start | bytes 1376260
  1.6 8.5 %collective-permute-start.1 = (f32[8,8,1,4,128]{4,1,3,2,0:T(8,128)S(1)}, f32[8,8,1,4,128]{4,1,3,2,0:T(8,128)S(1)}, u32[]{:S(2)}, u32[]{:S(2)}) collective-permute-start(f32[8,8,1,4,128]{4,1,3,2,0:T(8,128)S(1)} %copy.203), channel_id=1, source_target_pairs={{0,16},{1,17},{2,18},{3,19},{4,20},{5,21},{6,22},{7,23},{8,24},{9,... | collective-permute-start | bytes 393224 | tf_op jit(solution)/shard_map/ppermute | solution.py:16
  6.5 6.9 %collective-permute-start = (f32[8,8,1,4,128]{4,1,3,2,0:T(8,128)S(1)}, f32[8,8,1,4,128]{4,1,3,2,0:T(8,128)S(1)}, u32[]{:S(2)}, u32[]{:S(2)}) collective-permute-start(f32[8,8,1,4,128]{4,1,3,2,0:T(8,128)S(1)} %copy.203), channel_id=1, source_target_pairs={{16,0},{17,1},{18,2},{19,3},{20,4},{21,5},{22,6},{23,7},{24,8},{25... | collective-permute-start | bytes 393224 | tf_op jit(solution)/shard_map/ppermute | solution.py:19
  8.8 0.9 copy-start
  13.4 4.4 %collective-permute-start.2 = (f32[8,8,3,1,128]{4,1,3,2,0:T(8,128)S(1)}, f32[8,8,3,1,128]{4,1,3,2,0:T(8,128)S(1)}, u32[]{:S(2)}, u32[]{:S(2)}) collective-permute-start(f32[8,8,3,1,128]{4,1,3,2,0:T(8,128)S(1)} %get-tuple-element.286), channel_id=1, source_target_pairs={{4,0},{8,4},{12,8},{5,1},{9,5},{13,9},{6,2},{10,6},{14,10},{7,3},{... | collective-permute-start | bytes 294920 | tf_op jit(solution)/shard_map/ppermute | solution.py:19
  14.7 4.0 %collective-permute-start.3 = (f32[8,8,3,1,128]{4,1,3,2,0:T(8,128)S(1)}, f32[8,8,3,1,128]{4,1,3,2,0:T(8,128)S(1)}, u32[]{:S(2)}, u32[]{:S(2)}) collective-permute-start(f32[8,8,3,1,128]{4,1,3,2,0:T(8,128)S(1)} %get-tuple-element.285), channel_id=1, source_target_pairs={{0,4},{4,8},{8,12},{1,5},{5,9},{9,13},{2,6},{6,10},{10,14},{3,7},{... | collective-permute-start | bytes 294920 | tf_op jit(solution)/shard_map/ppermute | solution.py:16
  19.8 5.7 %collective-permute-start.5 = (f32[8,8,3,6,1]{1,0,4,3,2:T(8,128)S(1)}, f32[8,8,3,6,1]{1,0,4,3,2:T(8,128)S(1)}, u32[]{:S(2)}, u32[]{:S(2)}) collective-permute-start(f32[8,8,3,6,1]{1,0,4,3,2:T(8,128)S(1)} %copy.278), channel_id=1, source_target_pairs={{0,1},{1,2},{2,3},{4,5},{5,6},{6,7},{8,9},{9,10},{10,11},{12,13},{... | collective-permute-start | bytes 13832 | tf_op jit(solution)/shard_map/ppermute | solution.py:16
  24.2 6.5 %collective-permute-start.4 = (f32[8,8,3,6,1]{1,0,4,3,2:T(8,128)S(1)}, f32[8,8,3,6,1]{1,0,4,3,2:T(8,128)S(1)}, u32[]{:S(2)}, u32[]{:S(2)}) collective-permute-start(f32[8,8,3,6,1]{1,0,4,3,2:T(8,128)S(1)} %copy.277), channel_id=1, source_target_pairs={{1,0},{2,1},{3,2},{5,4},{6,5},{7,6},{9,8},{10,9},{11,10},{13,12},{... | collective-permute-start | bytes 13832 | tf_op jit(solution)/shard_map/ppermute | solution.py:19
  83.0 10.6 %collective-permute-start.6 = (f32[8,8,1,4,128]{4,1,3,0,2:T(8,128)S(1)}, f32[8,8,1,4,128]{4,1,3,0,2:T(8,128)S(1)}, u32[]{:S(2)}, u32[]{:S(2)}) collective-permute-start(f32[8,8,1,4,128]{4,1,3,0,2:T(8,128)S(1)} %bitcast.785), channel_id=1, source_target_pairs={{16,0},{17,1},{18,2},{19,3},{20,4},{21,5},{22,6},{23,7},{24,8},{25... | collective-permute-start | bytes 393224 | tf_op jit(solution)/shard_map/ppermute | solution.py:19
  84.3 9.3 %collective-permute-start.7 = (f32[8,8,1,4,128]{4,1,3,0,2:T(8,128)S(1)}, f32[8,8,1,4,128]{4,1,3,0,2:T(8,128)S(1)}, u32[]{:S(2)}, u32[]{:S(2)}) collective-permute-start(f32[8,8,1,4,128]{4,1,3,0,2:T(8,128)S(1)} %bitcast.786), channel_id=1, source_target_pairs={{0,16},{1,17},{2,18},{3,19},{4,20},{5,21},{6,22},{7,23},{8,24},{9,... | collective-permute-start | bytes 393224 | tf_op jit(solution)/shard_map/ppermute | solution.py:16
  90.1 0.7 copy-start.3
  93.7 4.4 %collective-permute-start.8 = (f32[8,8,3,1,128]{4,1,3,0,2:T(8,128)S(1)}, f32[8,8,3,1,128]{4,1,3,0,2:T(8,128)S(1)}, u32[]{:S(2)}, u32[]{:S(2)}) collective-permute-start(f32[8,8,3,1,128]{4,1,3,0,2:T(8,128)S(1)} %get-tuple-element.284), channel_id=1, source_target_pairs={{4,0},{8,4},{12,8},{5,1},{9,5},{13,9},{6,2},{10,6},{14,10},{7,3},{... | collective-permute-start | bytes 294920 | tf_op jit(solution)/shard_map/ppermute | solution.py:19
  95.0 4.0 %collective-permute-start.9 = (f32[8,8,3,1,128]{4,1,3,0,2:T(8,128)S(1)}, f32[8,8,3,1,128]{4,1,3,0,2:T(8,128)S(1)}, u32[]{:S(2)}, u32[]{:S(2)}) collective-permute-start(f32[8,8,3,1,128]{4,1,3,0,2:T(8,128)S(1)} %get-tuple-element.283), channel_id=1, source_target_pairs={{0,4},{4,8},{8,12},{1,5},{5,9},{9,13},{2,6},{6,10},{10,14},{3,7},{... | collective-permute-start | bytes 294920 | tf_op jit(solution)/shard_map/ppermute | solution.py:16
  100.1 4.5 %collective-permute-start.11 = (f32[8,8,3,6,1]{1,0,4,3,2:T(8,128)S(1)}, f32[8,8,3,6,1]{1,0,4,3,2:T(8,128)S(1)}, u32[]{:S(2)}, u32[]{:S(2)}) collective-permute-start(f32[8,8,3,6,1]{1,0,4,3,2:T(8,128)S(1)} %copy.218), channel_id=1, source_target_pairs={{0,1},{1,2},{2,3},{4,5},{5,6},{6,7},{8,9},{9,10},{10,11},{12,13},{... | collective-permute-start | bytes 13832 | tf_op jit(solution)/shard_map/ppermute | solution.py:16
  103.2 6.2 %collective-permute-start.10 = (f32[8,8,3,6,1]{1,0,4,3,2:T(8,128)S(1)}, f32[8,8,3,6,1]{1,0,4,3,2:T(8,128)S(1)}, u32[]{:S(2)}, u32[]{:S(2)}) collective-permute-start(f32[8,8,3,6,1]{1,0,4,3,2:T(8,128)S(1)} %copy.216), channel_id=1, source_target_pairs={{1,0},{2,1},{3,2},{5,4},{6,5},{7,6},{9,8},{10,9},{11,10},{13,12},{... | collective-permute-start | bytes 13832 | tf_op jit(solution)/shard_map/ppermute | solution.py:19
  161.4 7.3 %collective-permute-start.12 = (f32[8,8,1,4,128]{4,1,3,0,2:T(8,128)S(1)}, f32[8,8,1,4,128]{4,1,3,0,2:T(8,128)S(1)}, u32[]{:S(2)}, u32[]{:S(2)}) collective-permute-start(f32[8,8,1,4,128]{4,1,3,0,2:T(8,128)S(1)} %bitcast.802), channel_id=1, source_target_pairs={{16,0},{17,1},{18,2},{19,3},{20,4},{21,5},{22,6},{23,7},{24,8},{25... | collective-permute-start | bytes 393224 | tf_op jit(solution)/shard_map/ppermute | solution.py:19
  162.7 7.1 %collective-permute-start.13 = (f32[8,8,1,4,128]{4,1,3,0,2:T(8,128)S(1)}, f32[8,8,1,4,128]{4,1,3,0,2:T(8,128)S(1)}, u32[]{:S(2)}, u32[]{:S(2)}) collective-permute-start(f32[8,8,1,4,128]{4,1,3,0,2:T(8,128)S(1)} %bitcast.803), channel_id=1, source_target_pairs={{0,16},{1,17},{2,18},{3,19},{4,20},{5,21},{6,22},{7,23},{8,24},{9,... | collective-permute-start | bytes 393224 | tf_op jit(solution)/shard_map/ppermute | solution.py:16
  169.8 4.4 %collective-permute-start.14 = (f32[8,8,3,1,128]{4,1,3,0,2:T(8,128)S(1)}, f32[8,8,3,1,128]{4,1,3,0,2:T(8,128)S(1)}, u32[]{:S(2)}, u32[]{:S(2)}) collective-permute-start(f32[8,8,3,1,128]{4,1,3,0,2:T(8,128)S(1)} %get-tuple-element.282), channel_id=1, source_target_pairs={{4,0},{8,4},{12,8},{5,1},{9,5},{13,9},{6,2},{10,6},{14,10},{7,3},{... | collective-permute-start | bytes 294920 | tf_op jit(solution)/shard_map/ppermute | solution.py:19
  171.1 4.0 %collective-permute-start.15 = (f32[8,8,3,1,128]{4,1,3,0,2:T(8,128)S(1)}, f32[8,8,3,1,128]{4,1,3,0,2:T(8,128)S(1)}, u32[]{:S(2)}, u32[]{:S(2)}) collective-permute-start(f32[8,8,3,1,128]{4,1,3,0,2:T(8,128)S(1)} %get-tuple-element.281), channel_id=1, source_target_pairs={{0,4},{4,8},{8,12},{1,5},{5,9},{9,13},{2,6},{6,10},{10,14},{3,7},{... | collective-permute-start | bytes 294920 | tf_op jit(solution)/shard_map/ppermute | solution.py:16
  174.1 0.9 copy-start.2
  176.2 4.5 %collective-permute-start.17 = (f32[8,8,3,6,1]{1,0,4,3,2:T(8,128)S(1)}, f32[8,8,3,6,1]{1,0,4,3,2:T(8,128)S(1)}, u32[]{:S(2)}, u32[]{:S(2)}) collective-permute-start(f32[8,8,3,6,1]{1,0,4,3,2:T(8,128)S(1)} %copy.230), channel_id=1, source_target_pairs={{0,1},{1,2},{2,3},{4,5},{5,6},{6,7},{8,9},{9,10},{10,11},{12,13},{... | collective-permute-start | bytes 13832 | tf_op jit(solution)/shard_map/ppermute | solution.py:16
  179.3 6.2 %collective-permute-start.16 = (f32[8,8,3,6,1]{1,0,4,3,2:T(8,128)S(1)}, f32[8,8,3,6,1]{1,0,4,3,2:T(8,128)S(1)}, u32[]{:S(2)}, u32[]{:S(2)}) collective-permute-start(f32[8,8,3,6,1]{1,0,4,3,2:T(8,128)S(1)} %copy.228), channel_id=1, source_target_pairs={{1,0},{2,1},{3,2},{5,4},{6,5},{7,6},{9,8},{10,9},{11,10},{13,12},{... | collective-permute-start | bytes 13832 | tf_op jit(solution)/shard_map/ppermute | solution.py:19
where the time goes:
time: 247 us; the launch traced here: 246 us
  blocking collectives  129 us (52%)
  starting transfers between devices  42.5 us (17%)
  other arithmetic  23.9 us (10%)
  local copies, waits for them, and re-layouts  18.8 us (8%)
  waiting for transfers between devices  18.3 us (7%)
  matrix products  11.8 us (5%)
    psum x2, blocking collectives, shards(): summed = lax.psum(partial_sums, ('gx', 'gy', 'gz'))  87.7 us
    psum x1, blocking collectives, shards(): lax.psum((pair(rhs, rhs), pair(rhs, raw_image), pair(raw_image, raw_image...  41.6 us
    ppermute x9, starting transfers between devices, with_halo(): lax.ppermute(lax.slice_in_dim(block, block.shape[dim] - width, None, axis...  30.9 us
    ppermute x9, waiting for transfers between devices, with_halo(): lax.ppermute(lax.slice_in_dim(block, 0, width, axis=dim), axis, backward)  14.6 us
    ppermute x9, starting transfers between devices, with_halo(): lax.ppermute(lax.slice_in_dim(block, 0, width, axis=dim), axis, backward)  11.6 us
    another operation x12, other arithmetic, normalizer(): lower = jnp.linalg.cholesky(gram)  5.63 us
    unnamed x14, local copies, waits for them, and re-layouts  5.27 us
    dot_general x11, matrix products, mix(): return jnp.einsum('asxyz,sr->arxyz', field, matrix, precision=HIGH)  4.97 us
  transfers between devices with their start and end apart: 18, of which 8 were waited for; matrix products, arithmetic and copies ran while one was open for 5% of the time, Pallas kernels for 0%

commit v1 on v0

--- a/solution.py
+++ b/solution.py
@@ -80,7 +80,7 @@
         else:
             stacked = jnp.stack(basis + [image])
             partial_sums = jnp.einsum("karxyz,asxyz->krs", stacked, image, precision=HIGH)
-            summed = lax.psum(partial_sums, ("gx", "gy", "gz"))
+            summed = lax.psum(lax.psum(partial_sums, ("gy", "gz")), "gx")
             coeffs = [summed[index] for index in range(len(basis))]
             gram = summed[len(basis)]
         rest = image

time: 247 us -> 296 us (1.20)
  blocking collectives: 129 us -> 177 us
    psum x2 -> x4, blocking collectives: 87.7 us -> 136 us  [shards(): summed = lax.psum(lax.psum(partial_sums, ('gy', 'gz')), 'gx')]
  transfers between devices with their start and end apart: 18 -> 18, of which waited for: 8 -> 8; matrix products, arithmetic and copies ran while one was open for 5% -> 4% of each run, Pallas kernels for 0% -> 0%
where the time goes in v1:
time: 296 us; the launch traced here: 293 us
  blocking collectives  177 us (60%)
  starting transfers between devices  41.7 us (14%)
  other arithmetic  23.7 us (8%)
  local copies, waits for them, and re-layouts  18.7 us (6%)
  waiting for transfers between devices  18.3 us (6%)
  matrix products  11.8 us (4%)
    psum x4, blocking collectives, shards(): summed = lax.psum(lax.psum(partial_sums, ('gy', 'gz')), 'gx')  136 us
    psum x1, blocking collectives, shards(): lax.psum((pair(rhs, rhs), pair(rhs, raw_image), pair(raw_image, raw_image...  41.6 us
    ppermute x9, starting transfers between devices, with_halo(): lax.ppermute(lax.slice_in_dim(block, block.shape[dim] - width, None, axis...  30 us
    ppermute x9, waiting for transfers between devices, with_halo(): lax.ppermute(lax.slice_in_dim(block, 0, width, axis=dim), axis, backward)  14.6 us
    ppermute x9, starting transfers between devices, with_halo(): lax.ppermute(lax.slice_in_dim(block, 0, width, axis=dim), axis, backward)  11.6 us
  transfers between devices with their start and end apart: 18, of which 8 were waited for; matrix products, arithmetic and copies ran while one was open for 4% of the time, Pallas kernels for 0%

profile of v1, /device:TPU:0, one launch (start us, length us, event | category | flops | bytes accessed | tf_op | source)
XLA Modules:
  0.0 293.0 jit_solution(1551030800274486974)
XLA Ops:
  0.6 1.0 copy.203
  1.6 4.9 %collective-permute-start.1 = (f32[8,8,1,4,128]{4,1,3,2,0:T(8,128)S(1)}, f32[8,8,1,4,128]{4,1,3,2,0:T(8,128)S(1)}, u32[]{:S(2)}, u32[]{:S(2)}) collective-permute-start(f32[8,8,1,4,128]{4,1,3,2,0:T(8,128)S(1)} %copy.203), channel_id=1, source_target_pairs={{0,16},{1,17},{2,18},{3,19},{4,20},{5,21},{6,22},{7,23},{8,24},{9,... | collective-permute-start | bytes 393224 | tf_op jit(solution)/shard_map/ppermute | solution.py:16
  6.5 1.3 collective-permute-start
  10.2 3.1 %collective-permute-done = f32[8,8,1,4,128]{4,1,3,2,0:T(8,128)S(1)} collective-permute-done((f32[8,8,1,4,128]{4,1,3,2,0:T(8,128)S(1)}, f32[8,8,1,4,128]{4,1,3,2,0:T(8,128)S(1)}, u32[]{:S(2)}, u32[]{:S(2)}) %collective-permute-start) | collective-permute-done | bytes 131104 | tf_op jit(solution)/shard_map/ppermute | solution.py:19
  13.4 1.3 collective-permute-start.2
  14.7 3.0 %collective-permute-start.3 = (f32[8,8,3,1,128]{4,1,3,2,0:T(8,128)S(1)}, f32[8,8,3,1,128]{4,1,3,2,0:T(8,128)S(1)}, u32[]{:S(2)}, u32[]{:S(2)}) collective-permute-start(f32[8,8,3,1,128]{4,1,3,2,0:T(8,128)S(1)} %get-tuple-element.285), channel_id=1, source_target_pairs={{0,4},{4,8},{8,12},{1,5},{5,9},{9,13},{2,6},{6,10},{10,14},{3,7},{... | collective-permute-start | bytes 294920 | tf_op jit(solution)/shard_map/ppermute | solution.py:16
  19.8 3.5 %collective-permute-start.5 = (f32[8,8,3,6,1]{1,0,4,3,2:T(8,128)S(1)}, f32[8,8,3,6,1]{1,0,4,3,2:T(8,128)S(1)}, u32[]{:S(2)}, u32[]{:S(2)}) collective-permute-start(f32[8,8,3,6,1]{1,0,4,3,2:T(8,128)S(1)} %copy.278), channel_id=1, source_target_pairs={{0,1},{1,2},{2,3},{4,5},{5,6},{6,7},{8,9},{9,10},{10,11},{12,13},{... | collective-permute-start | bytes 13832 | tf_op jit(solution)/shard_map/ppermute | solution.py:16
  24.2 1.3 collective-permute-start.4
  25.6 0.9 copy.209
  26.7 4.0 %collective-permute-done.4 = f32[8,8,3,6,1]{1,0,4,3,2:T(8,128)S(1)} collective-permute-done((f32[8,8,3,6,1]{1,0,4,3,2:T(8,128)S(1)}, f32[8,8,3,6,1]{1,0,4,3,2:T(8,128)S(1)}, u32[]{:S(2)}, u32[]{:S(2)}) %collective-permute-start.4) | collective-permute-done | bytes 4640 | tf_op jit(solution)/shard_map/ppermute | solution.py:19
  30.7 0.9 copy.207
  31.8 1.0 multiply_add_fusion.2
  33.6 41.6 %all-reduce.1 = (f32[8,8]{0,1:T(8,128)S(1)}, f32[8,8]{1,0:T(8,128)S(1)}, f32[8,8]{0,1:T(8,128)S(1)}) all-reduce(f32[8,8]{0,1:T(8,128)S(1)} %convolution_bitcast_fusion.13, f32[8,8]{1,0:T(8,128)S(1)} %convolution_bitcast_fusion.12, f32[8,8]{0,1:T(8,128)S(1)} %convolution_bitcast_fusion.11), channel_id=1, replica_groups=mesh['gx'=2,'gy'=4,'gz'=4] {'gx','gy','gz'}, use_global_device_ids=true, to_apply=%region_0.0 | all-reduce | flops 192 | bytes 1536 | tf_op jit(solution)/shard_map/psum | solution.py:66
  83.0 1.3 collective-permute-start.6
  84.3 4.6 %collective-permute-start.7 = (f32[8,8,1,4,128]{4,1,3,0,2:T(8,128)S(1)}, f32[8,8,1,4,128]{4,1,3,0,2:T(8,128)S(1)}, u32[]{:S(2)}, u32[]{:S(2)}) collective-permute-start(f32[8,8,1,4,128]{4,1,3,0,2:T(8,128)S(1)} %bitcast.786), channel_id=1, source_target_pairs={{0,16},{1,17},{2,18},{3,19},{4,20},{5,21},{6,22},{7,23},{8,24},{9,... | collective-permute-start | bytes 393224 | tf_op jit(solution)/shard_map/ppermute | solution.py:16
  90.8 2.7 and_reduce_fusion
  93.5 1.3 collective-permute-start.8
  94.8 3.0 %collective-permute-start.9 = (f32[8,8,3,1,128]{4,1,3,0,2:T(8,128)S(1)}, f32[8,8,3,1,128]{4,1,3,0,2:T(8,128)S(1)}, u32[]{:S(2)}, u32[]{:S(2)}) collective-permute-start(f32[8,8,3,1,128]{4,1,3,0,2:T(8,128)S(1)} %get-tuple-element.283), channel_id=1, source_target_pairs={{0,4},{4,8},{8,12},{1,5},{5,9},{9,13},{2,6},{6,10},{10,14},{3,7},{... | collective-permute-start | bytes 294920 | tf_op jit(solution)/shard_map/ppermute | solution.py:16
  99.1 0.9 copy.218
  100.0 2.2 collective-permute-start.11
  103.0 1.3 collective-permute-start.10
  104.4 0.9 copy.219
  105.6 3.7 %collective-permute-done.10 = f32[8,8,3,6,1]{1,0,4,3,2:T(8,128)S(1)} collective-permute-done((f32[8,8,3,6,1]{1,0,4,3,2:T(8,128)S(1)}, f32[8,8,3,6,1]{1,0,4,3,2:T(8,128)S(1)}, u32[]{:S(2)}, u32[]{:S(2)}) %collective-permute-start.10) | collective-permute-done | bytes 4640 | tf_op jit(solution)/shard_map/ppermute | solution.py:19
  109.3 0.9 copy.217
  110.5 1.1 multiply_add_fusion.1
  111.5 1.6 convolution_bitcast_fusion.7
  113.2 60.0 %psum.52 = f32[3,8,8]{2,1,0:T(8,128)S(1)} all-reduce(f32[3,8,8]{2,1,0:T(8,128)S(1)} %convolution_bitcast_fusion.7), channel_id=1, replica_groups=mesh['gx'=2,'gy'=4,'gz'=4] {'gy','gz'}, use_global_device_ids=true, to_apply=%region_5.8 | all-reduce | flops 192 | bytes 1536 | tf_op jit(solution)/shard_map/psum | solution.py:83
  173.2 6.9 %psum.53 = f32[3,8,8]{2,1,0:T(8,128)S(1)} all-reduce(f32[3,8,8]{2,1,0:T(8,128)S(1)} %psum.52), channel_id=1, replica_groups=mesh['gx'=2,'gy'=4,'gz'=4] {'gx'}, use_global_device_ids=true, to_apply=%region_6.9 | all-reduce | flops 192 | bytes 1536 | tf_op jit(solution)/shard_map/psum | solution.py:83
  183.8 1.3 fusion.3
  185.4 1.3 collective-permute-start.12
  186.7 4.6 %collective-permute-start.13 = (f32[8,8,1,4,128]{4,1,3,0,2:T(8,128)S(1)}, f32[8,8,1,4,128]{4,1,3,0,2:T(8,128)S(1)}, u32[]{:S(2)}, u32[]{:S(2)}) collective-permute-start(f32[8,8,1,4,128]{4,1,3,0,2:T(8,128)S(1)} %bitcast.803), channel_id=1, source_target_pairs={{0,16},{1,17},{2,18},{3,19},{4,20},{5,21},{6,22},{7,23},{8,24},{9,... | collective-permute-start | bytes 393224 | tf_op jit(solution)/shard_map/ppermute | solution.py:16
  191.3 1.3 fusion.499
  192.7 1.1 collective-permute-done.13
  193.8 1.3 collective-permute-start.14
  195.1 3.0 %collective-permute-start.15 = (f32[8,8,3,1,128]{4,1,3,0,2:T(8,128)S(1)}, f32[8,8,3,1,128]{4,1,3,0,2:T(8,128)S(1)}, u32[]{:S(2)}, u32[]{:S(2)}) collective-permute-start(f32[8,8,3,1,128]{4,1,3,0,2:T(8,128)S(1)} %get-tuple-element.281), channel_id=1, source_target_pairs={{0,4},{4,8},{8,12},{1,5},{5,9},{9,13},{2,6},{6,10},{10,14},{3,7},{... | collective-permute-start | bytes 294920 | tf_op jit(solution)/shard_map/ppermute | solution.py:16
  199.3 0.9 copy.230
  200.2 1.3 collective-permute-start.17
  202.4 1.3 collective-permute-start.16
  203.8 0.9 copy.231
  205.0 3.7 %collective-permute-done.16 = f32[8,8,3,6,1]{1,0,4,3,2:T(8,128)S(1)} collective-permute-done((f32[8,8,3,6,1]{1,0,4,3,2:T(8,128)S(1)}, f32[8,8,3,6,1]{1,0,4,3,2:T(8,128)S(1)}, u32[]{:S(2)}, u32[]{:S(2)}) %collective-permute-start.16) | collective-permute-done | bytes 4640 | tf_op jit(solution)/shard_map/ppermute | solution.py:19
  208.7 0.9 copy.229
  209.9 1.0 multiply_add_fusion
  210.9 1.6 convolution_bitcast_fusion.6
  212.5 59.7 %psum.54 = f32[4,8,8]{2,1,0:T(8,128)S(1)} all-reduce(f32[4,8,8]{2,1,0:T(8,128)S(1)} %convolution_bitcast_fusion.6), channel_id=1, replica_groups=mesh['gx'=2,'gy'=4,'gz'=4] {'gy','gz'}, use_global_device_ids=true, to_apply=%region_7.10 | all-reduce | flops 256 | bytes 2048 | tf_op jit(solution)/shard_map/psum | solution.py:83
  272.2 9.1 %psum.55 = f32[4,8,8]{2,1,0:T(8,128)S(1)} all-reduce(f32[4,8,8]{2,1,0:T(8,128)S(1)} %psum.54), channel_id=1, replica_groups=mesh['gx'=2,'gy'=4,'gz'=4] {'gx'}, use_global_device_ids=true, to_apply=%region_8.11 | all-reduce | flops 256 | bytes 2048 | tf_op jit(solution)/shard_map/psum | solution.py:83
  285.6 1.1 fusion.7
  287.0 0.9 copy.245
  287.9 3.2 %fusion.498 = f32[4,8,3,8]{3,1,2,0:T(8,128)} fusion(f32[4,8,3,8]{3,1,2,0:T(8,128)} %copy-done.2, s32[]{:T(128)} %bitcast.379, s32[]{:T(128)} %bitcast.380, f32[4,8,8]{2,1,0:T(8,128)S(1)} %psum.55, pred[]{:T(512)} %get-tuple-element.118), kind=kLoop, calls=%fused_computation.797 | loop fusion | flops 64 | bytes 9984 | tf_op jit(solution)/shard_map/scatter | solution.py:94
  (151 shorter events, 31.8 us)
Async XLA Ops:
  0.6 8.1 %copy-start.1 = (bf16[7,8,8,1,4,128]{5,4,3,2,1,0:T(4,128)(2,1)S(1)}, bf16[7,8,8,1,4,128]{5,4,3,2,1,0:T(4,128)(2,1)}, u32[]{:S(2)}) copy-start(bf16[7,8,8,1,4,128]{5,4,3,2,1,0:T(4,128)(2,1)} %param.24) | copy-start | bytes 1376260
  1.6 8.5 %collective-permute-start.1 = (f32[8,8,1,4,128]{4,1,3,2,0:T(8,128)S(1)}, f32[8,8,1,4,128]{4,1,3,2,0:T(8,128)S(1)}, u32[]{:S(2)}, u32[]{:S(2)}) collective-permute-start(f32[8,8,1,4,128]{4,1,3,2,0:T(8,128)S(1)} %copy.203), channel_id=1, source_target_pairs={{0,16},{1,17},{2,18},{3,19},{4,20},{5,21},{6,22},{7,23},{8,24},{9,... | collective-permute-start | bytes 393224 | tf_op jit(solution)/shard_map/ppermute | solution.py:16
  6.5 6.9 %collective-permute-start = (f32[8,8,1,4,128]{4,1,3,2,0:T(8,128)S(1)}, f32[8,8,1,4,128]{4,1,3,2,0:T(8,128)S(1)}, u32[]{:S(2)}, u32[]{:S(2)}) collective-permute-start(f32[8,8,1,4,128]{4,1,3,2,0:T(8,128)S(1)} %copy.203), channel_id=1, source_target_pairs={{16,0},{17,1},{18,2},{19,3},{20,4},{21,5},{22,6},{23,7},{24,8},{25... | collective-permute-start | bytes 393224 | tf_op jit(solution)/shard_map/ppermute | solution.py:19
  8.8 0.9 copy-start
  13.4 4.4 %collective-permute-start.2 = (f32[8,8,3,1,128]{4,1,3,2,0:T(8,128)S(1)}, f32[8,8,3,1,128]{4,1,3,2,0:T(8,128)S(1)}, u32[]{:S(2)}, u32[]{:S(2)}) collective-permute-start(f32[8,8,3,1,128]{4,1,3,2,0:T(8,128)S(1)} %get-tuple-element.286), channel_id=1, source_target_pairs={{4,0},{8,4},{12,8},{5,1},{9,5},{13,9},{6,2},{10,6},{14,10},{7,3},{... | collective-permute-start | bytes 294920 | tf_op jit(solution)/shard_map/ppermute | solution.py:19
  14.7 4.0 %collective-permute-start.3 = (f32[8,8,3,1,128]{4,1,3,2,0:T(8,128)S(1)}, f32[8,8,3,1,128]{4,1,3,2,0:T(8,128)S(1)}, u32[]{:S(2)}, u32[]{:S(2)}) collective-permute-start(f32[8,8,3,1,128]{4,1,3,2,0:T(8,128)S(1)} %get-tuple-element.285), channel_id=1, source_target_pairs={{0,4},{4,8},{8,12},{1,5},{5,9},{9,13},{2,6},{6,10},{10,14},{3,7},{... | collective-permute-start | bytes 294920 | tf_op jit(solution)/shard_map/ppermute | solution.py:16
  19.8 5.7 %collective-permute-start.5 = (f32[8,8,3,6,1]{1,0,4,3,2:T(8,128)S(1)}, f32[8,8,3,6,1]{1,0,4,3,2:T(8,128)S(1)}, u32[]{:S(2)}, u32[]{:S(2)}) collective-permute-start(f32[8,8,3,6,1]{1,0,4,3,2:T(8,128)S(1)} %copy.278), channel_id=1, source_target_pairs={{0,1},{1,2},{2,3},{4,5},{5,6},{6,7},{8,9},{9,10},{10,11},{12,13},{... | collective-permute-start | bytes 13832 | tf_op jit(solution)/shard_map/ppermute | solution.py:16
  24.2 6.5 %collective-permute-start.4 = (f32[8,8,3,6,1]{1,0,4,3,2:T(8,128)S(1)}, f32[8,8,3,6,1]{1,0,4,3,2:T(8,128)S(1)}, u32[]{:S(2)}, u32[]{:S(2)}) collective-permute-start(f32[8,8,3,6,1]{1,0,4,3,2:T(8,128)S(1)} %copy.277), channel_id=1, source_target_pairs={{1,0},{2,1},{3,2},{5,4},{6,5},{7,6},{9,8},{10,9},{11,10},{13,12},{... | collective-permute-start | bytes 13832 | tf_op jit(solution)/shard_map/ppermute | solution.py:19
  83.0 10.5 %collective-permute-start.6 = (f32[8,8,1,4,128]{4,1,3,0,2:T(8,128)S(1)}, f32[8,8,1,4,128]{4,1,3,0,2:T(8,128)S(1)}, u32[]{:S(2)}, u32[]{:S(2)}) collective-permute-start(f32[8,8,1,4,128]{4,1,3,0,2:T(8,128)S(1)} %bitcast.785), channel_id=1, source_target_pairs={{16,0},{17,1},{18,2},{19,3},{20,4},{21,5},{22,6},{23,7},{24,8},{25... | collective-permute-start | bytes 393224 | tf_op jit(solution)/shard_map/ppermute | solution.py:19
  84.3 9.2 %collective-permute-start.7 = (f32[8,8,1,4,128]{4,1,3,0,2:T(8,128)S(1)}, f32[8,8,1,4,128]{4,1,3,0,2:T(8,128)S(1)}, u32[]{:S(2)}, u32[]{:S(2)}) collective-permute-start(f32[8,8,1,4,128]{4,1,3,0,2:T(8,128)S(1)} %bitcast.786), channel_id=1, source_target_pairs={{0,16},{1,17},{2,18},{3,19},{4,20},{5,21},{6,22},{7,23},{8,24},{9,... | collective-permute-start | bytes 393224 | tf_op jit(solution)/shard_map/ppermute | solution.py:16
  90.1 0.7 copy-start.3
  93.5 4.4 %collective-permute-start.8 = (f32[8,8,3,1,128]{4,1,3,0,2:T(8,128)S(1)}, f32[8,8,3,1,128]{4,1,3,0,2:T(8,128)S(1)}, u32[]{:S(2)}, u32[]{:S(2)}) collective-permute-start(f32[8,8,3,1,128]{4,1,3,0,2:T(8,128)S(1)} %get-tuple-element.284), channel_id=1, source_target_pairs={{4,0},{8,4},{12,8},{5,1},{9,5},{13,9},{6,2},{10,6},{14,10},{7,3},{... | collective-permute-start | bytes 294920 | tf_op jit(solution)/shard_map/ppermute | solution.py:19
  94.8 4.0 %collective-permute-start.9 = (f32[8,8,3,1,128]{4,1,3,0,2:T(8,128)S(1)}, f32[8,8,3,1,128]{4,1,3,0,2:T(8,128)S(1)}, u32[]{:S(2)}, u32[]{:S(2)}) collective-permute-start(f32[8,8,3,1,128]{4,1,3,0,2:T(8,128)S(1)} %get-tuple-element.283), channel_id=1, source_target_pairs={{0,4},{4,8},{8,12},{1,5},{5,9},{9,13},{2,6},{6,10},{10,14},{3,7},{... | collective-permute-start | bytes 294920 | tf_op jit(solution)/shard_map/ppermute | solution.py:16
  100.0 4.5 %collective-permute-start.11 = (f32[8,8,3,6,1]{1,0,4,3,2:T(8,128)S(1)}, f32[8,8,3,6,1]{1,0,4,3,2:T(8,128)S(1)}, u32[]{:S(2)}, u32[]{:S(2)}) collective-permute-start(f32[8,8,3,6,1]{1,0,4,3,2:T(8,128)S(1)} %copy.218), channel_id=1, source_target_pairs={{0,1},{1,2},{2,3},{4,5},{5,6},{6,7},{8,9},{9,10},{10,11},{12,13},{... | collective-permute-start | bytes 13832 | tf_op jit(solution)/shard_map/ppermute | solution.py:16
  103.0 6.2 %collective-permute-start.10 = (f32[8,8,3,6,1]{1,0,4,3,2:T(8,128)S(1)}, f32[8,8,3,6,1]{1,0,4,3,2:T(8,128)S(1)}, u32[]{:S(2)}, u32[]{:S(2)}) collective-permute-start(f32[8,8,3,6,1]{1,0,4,3,2:T(8,128)S(1)} %copy.216), channel_id=1, source_target_pairs={{1,0},{2,1},{3,2},{5,4},{6,5},{7,6},{9,8},{10,9},{11,10},{13,12},{... | collective-permute-start | bytes 13832 | tf_op jit(solution)/shard_map/ppermute | solution.py:19
  185.4 7.3 %collective-permute-start.12 = (f32[8,8,1,4,128]{4,1,3,0,2:T(8,128)S(1)}, f32[8,8,1,4,128]{4,1,3,0,2:T(8,128)S(1)}, u32[]{:S(2)}, u32[]{:S(2)}) collective-permute-start(f32[8,8,1,4,128]{4,1,3,0,2:T(8,128)S(1)} %bitcast.802), channel_id=1, source_target_pairs={{16,0},{17,1},{18,2},{19,3},{20,4},{21,5},{22,6},{23,7},{24,8},{25... | collective-permute-start | bytes 393224 | tf_op jit(solution)/shard_map/ppermute | solution.py:19
  186.7 7.1 %collective-permute-start.13 = (f32[8,8,1,4,128]{4,1,3,0,2:T(8,128)S(1)}, f32[8,8,1,4,128]{4,1,3,0,2:T(8,128)S(1)}, u32[]{:S(2)}, u32[]{:S(2)}) collective-permute-start(f32[8,8,1,4,128]{4,1,3,0,2:T(8,128)S(1)} %bitcast.803), channel_id=1, source_target_pairs={{0,16},{1,17},{2,18},{3,19},{4,20},{5,21},{6,22},{7,23},{8,24},{9,... | collective-permute-start | bytes 393224 | tf_op jit(solution)/shard_map/ppermute | solution.py:16
  193.8 4.4 %collective-permute-start.14 = (f32[8,8,3,1,128]{4,1,3,0,2:T(8,128)S(1)}, f32[8,8,3,1,128]{4,1,3,0,2:T(8,128)S(1)}, u32[]{:S(2)}, u32[]{:S(2)}) collective-permute-start(f32[8,8,3,1,128]{4,1,3,0,2:T(8,128)S(1)} %get-tuple-element.282), channel_id=1, source_target_pairs={{4,0},{8,4},{12,8},{5,1},{9,5},{13,9},{6,2},{10,6},{14,10},{7,3},{... | collective-permute-start | bytes 294920 | tf_op jit(solution)/shard_map/ppermute | solution.py:19
  195.1 4.0 %collective-permute-start.15 = (f32[8,8,3,1,128]{4,1,3,0,2:T(8,128)S(1)}, f32[8,8,3,1,128]{4,1,3,0,2:T(8,128)S(1)}, u32[]{:S(2)}, u32[]{:S(2)}) collective-permute-start(f32[8,8,3,1,128]{4,1,3,0,2:T(8,128)S(1)} %get-tuple-element.281), channel_id=1, source_target_pairs={{0,4},{4,8},{8,12},{1,5},{5,9},{9,13},{2,6},{6,10},{10,14},{3,7},{... | collective-permute-start | bytes 294920 | tf_op jit(solution)/shard_map/ppermute | solution.py:16
  198.1 0.9 copy-start.2
  200.2 3.6 %collective-permute-start.17 = (f32[8,8,3,6,1]{1,0,4,3,2:T(8,128)S(1)}, f32[8,8,3,6,1]{1,0,4,3,2:T(8,128)S(1)}, u32[]{:S(2)}, u32[]{:S(2)}) collective-permute-start(f32[8,8,3,6,1]{1,0,4,3,2:T(8,128)S(1)} %copy.230), channel_id=1, source_target_pairs={{0,1},{1,2},{2,3},{4,5},{5,6},{6,7},{8,9},{9,10},{10,11},{12,13},{... | collective-permute-start | bytes 13832 | tf_op jit(solution)/shard_map/ppermute | solution.py:16
  202.4 6.2 %collective-permute-start.16 = (f32[8,8,3,6,1]{1,0,4,3,2:T(8,128)S(1)}, f32[8,8,3,6,1]{1,0,4,3,2:T(8,128)S(1)}, u32[]{:S(2)}, u32[]{:S(2)}) collective-permute-start(f32[8,8,3,6,1]{1,0,4,3,2:T(8,128)S(1)} %copy.228), channel_id=1, source_target_pairs={{1,0},{2,1},{3,2},{5,4},{6,5},{7,6},{9,8},{10,9},{11,10},{13,12},{... | collective-permute-start | bytes 13832 | tf_op jit(solution)/shard_map/ppermute | solution.py:19
